TPU v7x, 32 devices: a whole 2x2x4 slice. The times are simulated.
32 devices in a mesh: dp: 8 (over y, x, core), tensor: 4 (over z).
Axes of the slice: x: 2, y: 2, z: 4, core: 2. Of those that a mesh axis runs over, the one named last changes fastest.
Arguments:
- hidden_in: bfloat16 [1024, 2048], P('dp'), may hold values from -6 to 6
- attn_gain: float32 [2048], replicated, may hold values from 0.5 to 1.5
- query_weight: bfloat16 [2048, 2048], P('dp', 'tensor'), may hold values from -0.125 to 0.125
- key_weight: bfloat16 [2048, 2048], P('dp', 'tensor'), may hold values from -0.125 to 0.125
- value_weight: bfloat16 [2048, 2048], P('dp', 'tensor'), may hold values from -0.125 to 0.125
- output_weight: bfloat16 [2048, 2048], P('dp', 'tensor'), may hold values from -1.5 to 1.5
- query_gain: float32 [2048], P('tensor'), may hold values from 0.5 to 1.5
- key_gain: float32 [2048], P('tensor'), may hold values from 0.5 to 1.5
- moe_gain: float32 [2048], replicated, may hold values from 0.5 to 1.5
- expert_gate_up: bfloat16 [2048, 16, 2, 1024], P(None, 'dp', None, 'tensor'), may hold values from -0.125 to 0.125
- expert_down: bfloat16 [2048, 16, 1024], P(None, 'dp', 'tensor'), may hold values from -0.1875 to 0.1875
- experts: int32 [1024, 8], P('dp'), may hold values from 0 to 15, all different within a row
- gates: float32 [1024, 8], P('dp'), may hold values from 0.25 to 0.75
- anchor: int32 [1024], P('dp'), may hold values from 0 to 1023, each once
- lengths: int32 [4], replicated, may hold values from 1 to 512, 1024 in all
- cotangent: bfloat16 [1024, 2048], P('dp'), may hold values from -8 to 8
Outputs:
- output: bfloat16 [1024, 2048], P('dp')
- input_grad: float32 [1024, 2048], P('dp')
- query_grad: float32 [2048, 2048], P('dp', 'tensor')
- key_grad: float32 [2048, 2048], P('dp', 'tensor')
- value_grad: float32 [2048, 2048], P('dp', 'tensor')
- output_grad: float32 [2048, 2048], P('dp', 'tensor')
- gate_up_grad: float32 [2048, 16, 2, 1024], P(None, 'dp', None, 'tensor')
- down_grad: float32 [2048, 16, 1024], P(None, 'dp', 'tensor')
- attn_gain_grad: float32 [2048], P('dp')
- query_gain_grad: float32 [2048], P('dp')
- key_gain_grad: float32 [2048], P('dp')
- moe_gain_grad: float32 [2048], P('dp')
Inputs may be any that keep to these rules, and one draw needn't show every extreme that they name: `anchor`: each number appears once. The lengths sum to 1024; the longest is exactly 512. Each row names 8 different experts.
All inputs are finite; a program needn't handle non-finite values.
Results may differ from a plain program's by a relative error of at most 0.033.
Values may be sent and summed in bfloat16 or wider, within the bound.
A program may use at most 256 MiB of HBM per device.

v0:
```python
import jax
import jax.numpy as jnp
from jax import lax
from jax.sharding import PartitionSpec as P

D = 2048
HD = 128
TOPK = 8
EPSILON = 1e-05
ROPE_BASE = 10000.0
NEG_FILL = -1e30


def rms_norm(values, gain):
    return values * lax.rsqrt(jnp.mean(values * values, axis=-1, keepdims=True) + EPSILON) * gain


def norm_back(values, gain, grad_out):
    inv_rms = lax.rsqrt(jnp.mean(values * values, axis=-1, keepdims=True) + EPSILON)
    weighted = grad_out * gain
    grad_in = inv_rms * weighted - values * inv_rms**3 * jnp.mean(
        weighted * values, axis=-1, keepdims=True
    )
    return (grad_in, jnp.sum(grad_out * values * inv_rms, axis=0))


def locate(anchor, lengths):
    ends = jnp.cumsum(lengths)
    starts = ends - lengths
    docs = jnp.sum((anchor[:, None] >= ends[None, :]).astype(jnp.int32), axis=1)
    which = docs[:, None] == jnp.arange(lengths.shape[0], dtype=jnp.int32)[None, :]
    begins = jnp.sum(jnp.where(which, starts[None, :], 0), axis=1)
    return (docs, (anchor - begins).astype(jnp.int32))


def rotary(tensor, positions):
    half_dim = HD // 2
    freqs = ROPE_BASE ** (-2.0 * jnp.arange(half_dim, dtype=jnp.float32) / HD)
    angles = positions.astype(jnp.float32)[:, None] * freqs[None, :]
    cosine = jnp.cos(angles)[:, None, :]
    sine_part = jnp.sin(angles)[:, None, :]
    first_half = tensor[..., :half_dim]
    second_half = tensor[..., half_dim:]
    return jnp.concatenate(
        [
            first_half * cosine - second_half * sine_part,
            second_half * cosine + first_half * sine_part,
        ],
        axis=-1,
    )


def routing(expert_rows, gate_rows, num_exp, capacity):
    tok_count = expert_rows.shape[0]
    flat_ids = expert_rows.reshape(-1)
    one_hot = (flat_ids[:, None] == jnp.arange(num_exp, dtype=jnp.int32)[None, :]).astype(jnp.int32)
    earlier = jnp.cumsum(one_hot, axis=0) - one_hot
    slot_ids = jnp.sum(earlier * one_hot, axis=1)
    dest_rows = jnp.where(slot_ids < capacity, flat_ids * capacity + slot_ids, num_exp * capacity)
    pair_token = jnp.arange(tok_count * TOPK, dtype=jnp.int32) // TOPK
    slot_source = jnp.zeros((num_exp * capacity + 1,), jnp.int32).at[dest_rows].set(pair_token)
    slot_filled = jnp.zeros((num_exp * capacity + 1,), jnp.float32).at[dest_rows].set(1.0)
    slot_gate = (
        jnp.zeros((num_exp * capacity + 1,), jnp.float32).at[dest_rows].set(gate_rows.reshape(-1))
    )
    return (dest_rows, slot_source[:-1], slot_filled[:-1], slot_gate[:-1])


def pair_allowed(query_anchor, query_docs, key_anchor, key_docs):
    return (
        (query_docs[:, None] == key_docs[None, :]) & (key_anchor[None, :] <= query_anchor[:, None])
    )[None]


def contract_last(left, right):
    return lax.dot_general(
        left, right, (((1,), (1,)), ((), ())), preferred_element_type=jnp.float32
    )


def contract_first(left, right):
    return lax.dot_general(
        left, right, (((0,), (0,)), ((), ())), preferred_element_type=jnp.float32
    )


def shards(
    hidden_in,
    attn_gain,
    query_weight,
    key_weight,
    value_weight,
    output_weight,
    query_gain,
    key_gain,
    moe_gain,
    expert_gate_up,
    expert_down,
    experts,
    gates,
    anchor,
    lengths,
    cotangent,
):
    tok_rows = hidden_in.shape[0]
    head_local = query_weight.shape[1] // HD
    score_scale = HD ** (-0.5)
    f32 = jnp.float32
    bf16 = jnp.bfloat16
    n_dp = lax.axis_size("dp")
    exp_local = expert_down.shape[1]
    num_exp = exp_local * n_dp
    capacity = 9 * tok_rows * TOPK // (8 * num_exp)
    inputs = hidden_in.astype(f32)
    grad_out = cotangent.astype(f32)
    docs, positions = locate(anchor, lengths)
    normed = rms_norm(inputs, attn_gain).astype(bf16)
    query_full, key_full, value_full, output_full = (
        lax.all_gather(query_weight, "dp", axis=0, tiled=True),
        lax.all_gather(key_weight, "dp", axis=0, tiled=True),
        lax.all_gather(value_weight, "dp", axis=0, tiled=True),
        lax.all_gather(output_weight, "dp", axis=0, tiled=True),
    )
    query_raw = jnp.dot(normed, query_full, preferred_element_type=f32)
    key_raw = jnp.dot(normed, key_full, preferred_element_type=f32)
    value_raw = jnp.dot(normed, value_full, preferred_element_type=f32)
    squares = lax.psum(
        (jnp.sum(query_raw * query_raw, axis=1), jnp.sum(key_raw * key_raw, axis=1)), "tensor"
    )
    query_inv = lax.rsqrt(squares[0] / D + EPSILON)[:, None]
    key_inv = lax.rsqrt(squares[1] / D + EPSILON)[:, None]
    query_rows = rotary(
        (query_raw * query_inv * query_gain).reshape(tok_rows, head_local, HD), positions
    ).astype(bf16)
    key_rows = rotary(
        (key_raw * key_inv * key_gain).reshape(tok_rows, head_local, HD), positions
    ).astype(bf16)
    value_rows = value_raw.astype(bf16).reshape(tok_rows, head_local, HD)
    run_max = jnp.full((head_local, tok_rows), NEG_FILL, f32)
    run_acc = jnp.zeros((tok_rows, head_local, HD), f32)
    key_piece = lax.all_gather(key_rows, "dp", axis=0, tiled=True)
    value_piece = lax.all_gather(value_rows, "dp", axis=0, tiled=True)
    anchor_piece = lax.all_gather(anchor, "dp", axis=0, tiled=True)
    piece_docs, unused = locate(anchor_piece, lengths)
    allowed = pair_allowed(anchor, docs, anchor_piece, piece_docs)
    scores = score_scale * jnp.einsum(
        "qhd,khd->hqk", query_rows, key_piece, preferred_element_type=f32
    )
    new_max = jnp.maximum(run_max, jnp.max(jnp.where(allowed, scores, NEG_FILL), axis=2))
    factor = jnp.exp(run_max - new_max)
    attn_probs = jnp.where(allowed, jnp.exp(scores - new_max[:, :, None]), 0.0)
    new_sum = jnp.sum(attn_probs, axis=2)
    update = jnp.einsum(
        "hqk,khd->qhd", attn_probs.astype(bf16), value_piece, preferred_element_type=f32
    )
    run_max, run_sum, run_acc = (new_max, new_sum, run_acc * factor.T[:, :, None] + update)
    log_total = run_max + jnp.log(run_sum)
    attended = run_acc / run_sum.T[:, :, None]
    attended_low = attended.reshape(tok_rows, -1).astype(bf16)
    attn_sum = lax.psum(
        contract_last(attended_low, output_full).astype(jnp.bfloat16), "tensor"
    ).astype(jnp.float32)
    residual = inputs + attn_sum
    moe_in = rms_norm(residual, moe_gain).astype(bf16)
    dest_rows, slot_source, slot_filled, slot_gate = routing(experts, gates, num_exp, capacity)
    buffer_rows = (moe_in[slot_source] * slot_filled[:, None].astype(bf16)).reshape(
        num_exp, capacity, D
    )
    slot_grad = (
        (grad_out[slot_source] * (slot_gate * slot_filled)[:, None])
        .astype(bf16)
        .reshape(num_exp, capacity, D)
    )
    recv_rows, recv_grad = (
        lax.all_to_all(buffer_rows, "dp", split_axis=0, concat_axis=1, tiled=True),
        lax.all_to_all(slot_grad, "dp", split_axis=0, concat_axis=1, tiled=True),
    )
    gate_up = jnp.einsum("ecd,dezf->eczf", recv_rows, expert_gate_up, preferred_element_type=f32)
    gate_part = gate_up[:, :, 0]
    up_part = gate_up[:, :, 1]
    activated = (jax.nn.silu(gate_part) * up_part).astype(bf16)
    expert_out = jnp.einsum("ecf,def->ecd", activated, expert_down, preferred_element_type=f32)
    grad_down = jnp.einsum("ecd,ecf->def", recv_grad, activated, preferred_element_type=f32)
    grad_act = jnp.einsum("ecd,def->ecf", recv_grad, expert_down, preferred_element_type=f32)
    sigmoid_gate = jax.nn.sigmoid(gate_part)
    grad_gate = grad_act * up_part * sigmoid_gate * (1.0 + gate_part * (1.0 - sigmoid_gate))
    grad_up = grad_act * jax.nn.silu(gate_part)
    grad_gateup = jnp.stack([grad_gate, grad_up], axis=2).astype(bf16)
    grad_gateup_w = jnp.einsum("ecd,eczf->dezf", recv_rows, grad_gateup, preferred_element_type=f32)
    grad_buffer = jnp.einsum(
        "eczf,dezf->ecd", grad_gateup, expert_gate_up, preferred_element_type=f32
    )
    back_out, back_grad = (
        lax.all_to_all(
            expert_out.astype(jnp.bfloat16), "dp", split_axis=1, concat_axis=0, tiled=True
        ).astype(expert_out.dtype),
        lax.all_to_all(
            grad_buffer.astype(jnp.bfloat16), "dp", split_axis=1, concat_axis=0, tiled=True
        ).astype(grad_buffer.dtype),
    )
    width = back_out.shape[2]
    zero_row = jnp.zeros((1, width), f32)
    table_rows = jnp.concatenate([back_out.reshape(num_exp * capacity, width), zero_row], axis=0)
    combined = jnp.sum(
        table_rows[dest_rows].reshape(tok_rows, TOPK, width) * gates[:, :, None], axis=1
    )
    grad_table = jnp.concatenate([back_grad.reshape(num_exp * capacity, width), zero_row], axis=0)
    grad_moe_part = jnp.sum(grad_table[dest_rows].reshape(tok_rows, TOPK, width), axis=1)
    moe_sum, grad_moe_in = (
        lax.psum(combined.astype(jnp.bfloat16), "tensor").astype(jnp.float32),
        lax.psum(grad_moe_part.astype(jnp.bfloat16), "tensor").astype(jnp.float32),
    )
    output = (residual + moe_sum).astype(bf16)
    query_full, key_full, value_full, output_full = (
        lax.all_gather(query_weight, "dp", axis=0, tiled=True),
        lax.all_gather(key_weight, "dp", axis=0, tiled=True),
        lax.all_gather(value_weight, "dp", axis=0, tiled=True),
        lax.all_gather(output_weight, "dp", axis=0, tiled=True),
    )
    grad_norm_moe, grad_moe_gain = norm_back(residual, moe_gain, grad_moe_in)
    grad_resid = grad_out + grad_norm_moe
    grad_resid_low = grad_resid.astype(bf16)
    grad_output_w = contract_first(grad_resid_low, attended_low)
    grad_att_low = (
        jnp.dot(grad_resid_low, output_full, preferred_element_type=f32)
        .astype(bf16)
        .reshape(tok_rows, head_local, HD)
    )
    delta_rows = jnp.sum(grad_att_low.astype(f32) * attended, axis=2).T
    key_piece = lax.all_gather(key_rows, "dp", axis=0, tiled=True)
    value_piece = lax.all_gather(value_rows, "dp", axis=0, tiled=True)
    anchor_piece = lax.all_gather(anchor, "dp", axis=0, tiled=True)
    piece_docs, unused = locate(anchor_piece, lengths)
    allowed = pair_allowed(anchor, docs, anchor_piece, piece_docs)
    scores = score_scale * jnp.einsum(
        "qhd,khd->hqk", query_rows, key_piece, preferred_element_type=f32
    )
    attn_probs = jnp.where(allowed, jnp.exp(scores - log_total[:, :, None]), 0.0)
    grad_probs = jnp.einsum("qhd,khd->hqk", grad_att_low, value_piece, preferred_element_type=f32)
    grad_scores = (attn_probs * (grad_probs - delta_rows[:, :, None])).astype(bf16)
    grad_query_rot = score_scale * jnp.einsum(
        "hqk,khd->qhd", grad_scores, key_piece, preferred_element_type=f32
    )
    query_wide = lax.all_gather(
        query_rows.astype(f32).astype(jnp.bfloat16), "dp", axis=0, tiled=True
    ).astype(jnp.float32)
    gradatt_wide = lax.all_gather(
        grad_att_low.astype(f32).astype(jnp.bfloat16), "dp", axis=0, tiled=True
    ).astype(jnp.float32)
    logtot_piece = lax.all_gather(
        log_total.T.astype(jnp.bfloat16), "dp", axis=0, tiled=True
    ).astype(jnp.float32)
    delta_piece = lax.all_gather(
        delta_rows.T.astype(jnp.bfloat16), "dp", axis=0, tiled=True
    ).astype(jnp.float32)
    anchor_piece = lax.all_gather(anchor, "dp", axis=0, tiled=True)
    query_piece = query_wide.astype(bf16)
    gradatt_piece = gradatt_wide.astype(bf16)
    piece_docs, unused = locate(anchor_piece, lengths)
    allowed = pair_allowed(anchor_piece, piece_docs, anchor, docs)
    scores = score_scale * jnp.einsum(
        "qhd,khd->hqk", query_piece, key_rows, preferred_element_type=f32
    )
    attn_probs = jnp.where(allowed, jnp.exp(scores - logtot_piece.T[:, :, None]), 0.0)
    grad_value = jnp.einsum(
        "hqk,qhd->khd", attn_probs.astype(bf16), gradatt_piece, preferred_element_type=f32
    )
    grad_probs = jnp.einsum("qhd,khd->hqk", gradatt_piece, value_rows, preferred_element_type=f32)
    grad_scores = (attn_probs * (grad_probs - delta_piece.T[:, :, None])).astype(bf16)
    grad_key = score_scale * jnp.einsum(
        "hqk,qhd->khd", grad_scores, query_piece, preferred_element_type=f32
    )
    grad_query_hat = rotary(grad_query_rot, -positions).reshape(tok_rows, -1)
    grad_key_hat = rotary(grad_key, -positions).reshape(tok_rows, -1)
    weighted_query = grad_query_hat * query_gain
    weighted_key = grad_key_hat * key_gain
    quarter = query_gain.shape[0]
    gain_offset = lax.axis_index("tensor") * quarter
    query_gain_part = jnp.sum(grad_query_hat * query_raw * query_inv, axis=0)
    key_gain_part = jnp.sum(grad_key_hat * key_raw * key_inv, axis=0)
    query_gain_wide = lax.dynamic_update_slice_in_dim(
        jnp.zeros((D,), f32), query_gain_part, gain_offset, 0
    )
    key_gain_wide = lax.dynamic_update_slice_in_dim(
        jnp.zeros((D,), f32), key_gain_part, gain_offset, 0
    )
    cross = lax.psum(
        (
            jnp.sum(weighted_query * query_raw, axis=1),
            jnp.sum(weighted_key * key_raw, axis=1),
            query_gain_wide,
            key_gain_wide,
        ),
        "tensor",
    )
    grad_query_raw = (
        query_inv * weighted_query - query_raw * query_inv**3 * cross[0][:, None] / D
    ).astype(bf16)
    grad_key_raw = (key_inv * weighted_key - key_raw * key_inv**3 * cross[1][:, None] / D).astype(
        bf16
    )
    grad_value_low = grad_value.reshape(tok_rows, -1).astype(bf16)
    grad_query_w = contract_first(normed, grad_query_raw)
    grad_key_w = contract_first(normed, grad_key_raw)
    grad_value_w = contract_first(normed, grad_value_low)
    grad_normed = (
        contract_last(grad_query_raw, query_full)
        + contract_last(grad_key_raw, key_full)
        + contract_last(grad_value_low, value_full)
    )
    grad_normed_sum = lax.psum(grad_normed.astype(jnp.bfloat16), "tensor").astype(jnp.float32)
    grad_norm_attn, grad_attn_gain = norm_back(inputs, attn_gain, grad_normed_sum)
    input_grad = grad_resid + grad_norm_attn
    summed = (
        lax.psum_scatter(
            grad_query_w.astype(jnp.bfloat16), "dp", scatter_dimension=0, tiled=True
        ).astype(jnp.float32),
        lax.psum_scatter(
            grad_key_w.astype(jnp.bfloat16), "dp", scatter_dimension=0, tiled=True
        ).astype(jnp.float32),
        lax.psum_scatter(
            grad_value_w.astype(jnp.bfloat16), "dp", scatter_dimension=0, tiled=True
        ).astype(jnp.float32),
        lax.psum_scatter(
            grad_output_w.astype(jnp.bfloat16), "dp", scatter_dimension=0, tiled=True
        ).astype(jnp.float32),
        lax.psum_scatter(
            grad_attn_gain.astype(jnp.bfloat16), "dp", scatter_dimension=0, tiled=True
        ).astype(jnp.float32),
        lax.psum_scatter(
            cross[2].astype(jnp.bfloat16), "dp", scatter_dimension=0, tiled=True
        ).astype(jnp.float32),
        lax.psum_scatter(
            cross[3].astype(jnp.bfloat16), "dp", scatter_dimension=0, tiled=True
        ).astype(jnp.float32),
        lax.psum_scatter(
            grad_moe_gain.astype(jnp.bfloat16), "dp", scatter_dimension=0, tiled=True
        ).astype(jnp.float32),
    )
    return (
        output,
        input_grad,
        summed[0],
        summed[1],
        summed[2],
        summed[3],
        grad_gateup_w,
        grad_down,
        summed[4],
        summed[5],
        summed[6],
        summed[7],
    )


def solution(mesh):
    in_specs = (
        P("dp", None),
        P(),
        P("dp", "tensor"),
        P("dp", "tensor"),
        P("dp", "tensor"),
        P("dp", "tensor"),
        P("tensor"),
        P("tensor"),
        P(),
        P(None, "dp", None, "tensor"),
        P(None, "dp", "tensor"),
        P("dp", None),
        P("dp", None),
        P("dp"),
        P(),
        P("dp", None),
    )
    out_specs = (
        P("dp", None),
        P("dp", None),
        P("dp", "tensor"),
        P("dp", "tensor"),
        P("dp", "tensor"),
        P("dp", "tensor"),
        P(None, "dp", None, "tensor"),
        P(None, "dp", "tensor"),
        P("dp"),
        P("dp"),
        P("dp"),
        P("dp"),
    )
    return jax.shard_map(shards, mesh=mesh, in_specs=in_specs, out_specs=out_specs, check_vma=False)
```

profile of v0, /device:TPU:0, one launch (start us, length us, event | category | flops | bytes accessed | tf_op | source)
XLA Modules:
  0.0 867.9 jit_solution(12070746928078635573)
XLA Ops:
  15.4 25.0 %all-gather.10.cloned.1.call-done = bf16[2048,512]{1,0:T(8,128)(2,1)} async-done(((bf16[256,512]{1,0:T(8,128)(2,1)}), bf16[2048,512]{1,0:T(8,128)(2,1)}) %all-gather.10.cloned.1.call-update) | async-done | bytes 2097168 | tf_op jit(solution)/shard_map/all_gather | solution.py:119
  42.8 27.3 %all-gather.12.cloned.1.call-done = bf16[2048,512]{1,0:T(8,128)(2,1)} async-done(((bf16[256,512]{1,0:T(8,128)(2,1)}), bf16[2048,512]{1,0:T(8,128)(2,1)}) %all-gather.12.cloned.1.call-update) | async-done | bytes 2097168 | tf_op jit(solution)/shard_map/all_gather | solution.py:120
  72.3 11.7 %all-reduce.7 = (f32[128]{0:T(128)S(1)}, f32[128]{0:T(128)S(1)}) all-reduce(f32[128]{0:T(128)S(1)} %get-tuple-element.131, f32[128]{0:T(128)S(1)} %get-tuple-element.133), channel_id=1, replica_groups=mesh['dp'=8,'tensor'=4] {'tensor'}, use_global_device_ids=true, to_apply=%region_5.6 | all-reduce | flops 256 | bytes 2048 | tf_op jit(solution)/shard_map/psum | solution.py:127
  93.3 6.6 all-gather.16.cloned.1.call-done
  103.5 4.5 reduce-window.19
  109.0 4.3 scatter_custom_fusion
  113.3 4.3 scatter_custom_fusion.1
  117.7 4.3 scatter_custom_fusion.2
  123.3 6.8 gather_fusion.2
  130.1 6.5 multiply_convert_fusion
  136.6 4.8 all-to-all-start.2
  141.4 65.4 %all-gather = s32[8,1,128]{2,1,0:T(1,128)S(1)} all-gather(s32[1,1,128]{2,1,0:T(1,128)S(1)} %bitcast.187), channel_id=1, replica_groups=mesh['dp'=8,'tensor'=4] {'dp'}, dimensions={0}, use_global_device_ids=true | all-gather | bytes 4608 | tf_op jit(solution)/shard_map/all_gather | solution.py:143
  218.9 38.4 %all-reduce.14.cloned.1.call-done = bf16[128,2048]{1,0:T(8,128)(2,1)} async-done(((bf16[128,2048]{1,0:T(8,128)(2,1)}), bf16[128,2048]{1,0:T(8,128)(2,1)}) %all-reduce.14.cloned.1.call-update) | async-done | bytes 524304 | tf_op jit(solution)/shard_map/psum | solution.py:160
  260.4 5.9 gather_fusion
  266.3 4.9 broadcast_multiply_fusion
  271.2 4.6 all-to-all-start
  275.8 5.3 copy.180
  281.0 49.4 %all-to-all-done = bf16[16,72,2048]{2,1,0:T(8,128)(2,1)} async-done(((bf16[16,72,2048]{2,1,0:T(8,128)(2,1)}), bf16[16,72,2048]{2,1,0:T(8,128)(2,1)}, u32[]{:S(2)}, u32[]{:S(2)}) %all-to-all-start) | async-done | bytes 4718624 | tf_op jit(solution)/shard_map/all_to_all | solution.py:175
  340.2 4.3 bitcast_convert_fusion
  344.5 9.4 %copy.183 = bf16[2,576,2048]{2,0,1:T(2,128)(2,1)} copy(bf16[2,576,2048]{2,1,0:T(8,128)(2,1)} %bitcast_convert_fusion) | data formatting | bytes 9437184 | tf_op jit(solution)/shard_map/convert_element_type | solution.py:198
  353.8 5.0 all-to-all-start.3
  358.9 3.6 convolution_convert_fusion
  362.5 9.3 %copy.176 = bf16[2,576,2048]{2,0,1:T(2,128)(2,1)} copy(bf16[2,576,2048]{2,1,0:T(8,128)(2,1)} %convolution_convert_fusion) | data formatting | bytes 9437184 | tf_op jit(solution)/shard_map/convert_element_type | solution.py:195
  371.8 41.7 %all-to-all-done.3 = bf16[2,576,2048]{2,0,1:T(2,128)(2,1)} async-done(((bf16[2,576,2048]{2,0,1:T(2,128)(2,1)}), bf16[2,576,2048]{2,0,1:T(2,128)(2,1)}, u32[]{:S(2)}, u32[]{:S(2)}) %all-to-all-start.3) | async-done | bytes 4718624 | tf_op jit(solution)/shard_map/all_to_all | solution.py:197
  413.6 4.6 all-to-all-start.1
  419.4 60.7 %all_gather.49 = bf16[1024,4]{0,1:T(4,128)(2,1)S(1)} all-gather(bf16[128,4]{0,1:T(4,128)(2,1)S(1)} %copy-done.64), channel_id=1, replica_groups=mesh['dp'=8,'tensor'=4] {'dp'}, dimensions={0}, use_global_device_ids=true | all-gather | bytes 9216 | tf_op jit(solution)/shard_map/all_gather | solution.py:250
  480.1 4.5 copy.184
  484.6 5.0 pad_convert_fusion
  489.5 12.6 %gather_fusion.3 = f32[1024,2048]{1,0:T(8,128)} fusion(f32[1153,2048]{1,0:T(8,128)} %pad_convert_fusion, s32[1024]{0:T(1024)S(1)} %broadcast_clamp_fusion), kind=kCustom, calls=%fused_computation.3 | custom fusion | bytes 16781312 | tf_op jit(solution)/shard_map/gather | solution.py:208
  502.1 6.2 bitcast_reduce_fusion
  511.7 6.7 copy.177
  518.5 26.7 %all-reduce.16.cloned.1.call-done = bf16[128,2048]{1,0:T(8,128)(2,1)} async-done(((bf16[128,2048]{1,0:T(8,128)(2,1)}), bf16[128,2048]{1,0:T(8,128)(2,1)}) %all-reduce.16.cloned.1.call-update) | async-done | bytes 524304 | tf_op jit(solution)/shard_map/psum | solution.py:211
  550.7 7.3 pad_convert_fusion.1
  557.9 12.6 %gather_fusion.1 = f32[1024,2048]{1,0:T(8,128)} fusion(f32[1153,2048]{1,0:T(8,128)} %pad_convert_fusion.1, s32[1024]{0:T(1024)S(1)} %broadcast_clamp_fusion), kind=kCustom, calls=%fused_computation.1 | custom fusion | bytes 16781312 | tf_op jit(solution)/shard_map/gather | solution.py:205
  570.5 7.5 fusion
  578.1 8.9 %all_gather.51 = bf16[1024,4]{0,1:T(4,128)(2,1)S(1)} all-gather(bf16[128,4]{0,1:T(4,128)(2,1)S(1)} %convert_element_type.256), channel_id=1, replica_groups=mesh['dp'=8,'tensor'=4] {'dp'}, dimensions={0}, use_global_device_ids=true | all-gather | bytes 9216 | tf_op jit(solution)/shard_map/all_gather | solution.py:253
  587.0 3.6 fusion.22
  605.2 19.0 %all-reduce.6 = (f32[128]{0:T(128)}, f32[128]{0:T(128)S(1)}, bf16[2048]{0:T(1024)(128)(2,1)}, bf16[2048]{0:T(1024)(128)(2,1)}) all-reduce(f32[128]{0:T(128)S(1)} %get-tuple-element.79, f32[128]{0:T(128)} %get-tuple-element.77, f32[2048]{0:T(1024)S(1)} %dynamic_update_slice.6, ...), channel_id=1, replica_groups=mesh['dp'=8,'tensor'=4] {'tensor'}, use_global_device_ids=true, to_apply=%region_26.27 | all-reduce | flops 4352 | bytes 26624 | tf_op jit(solution)/shard_map/psum | solution.py:287
  645.2 8.2 convolution_bitcast_fusion
  653.4 13.3 %copy.195 = f32[2048,2,2,256]{3,2,1,0:T(2,128)} copy(f32[2048,2,2,256]{0,3,2,1:T(8,128)} %convolution_bitcast_fusion) | data formatting | bytes 16777216
  666.6 6.2 convolution_bitcast_fusion.1
  672.9 7.2 copy.196
  684.0 24.2 %all-reduce.8 = (bf16[2048]{0:T(1024)(128)(2,1)S(1)}, bf16[2048]{0:T(1024)(128)(2,1)S(1)}, bf16[2048]{0:T(1024)(128)(2,1)S(1)}, bf16[2048]{0:T(1024)(128)(2,1)S(1)}) all-reduce(bf16[2048]{0:T(1024)(128)(2,1)S(1)} %get-tuple-element.74, bf16[2048]{0:T(1024)(128)(2,1)S(1)} %copy-done.65, ...), channel_id=6, replica_groups=mesh['dp'=8,'tensor'=4] {'dp'}, use_global_device_ids=true, to_apply=%region_36.37.clone | all-reduce | flops 8192 | bytes 32768
  710.8 3.7 fusion.24
  714.5 11.6 %reduce-scatter.11.cloned.1.call-done = bf16[256,512]{1,0:T(8,128)(2,1)} async-done(((bf16[2048,512]{1,0:T(8,128)(2,1)}), bf16[256,512]{1,0:T(8,128)(2,1)}) %reduce-scatter.11.cloned.1.call-update) | async-done | bytes 262160 | tf_op jit(solution)/shard_map/reduce_scatter | solution.py:324
  727.9 42.6 %reduce-scatter.9.cloned.1.call-done = bf16[256,512]{1,0:T(8,128)(2,1)} async-done(((bf16[2048,512]{1,0:T(8,128)(2,1)}), bf16[256,512]{1,0:T(8,128)(2,1)}) %reduce-scatter.9.cloned.1.call-update) | async-done | bytes 262160 | tf_op jit(solution)/shard_map/reduce_scatter | solution.py:321
  772.4 42.5 %reduce-scatter.7.cloned.1.call-done = bf16[256,512]{1,0:T(8,128)(2,1)} async-done(((bf16[2048,512]{1,0:T(8,128)(2,1)}), bf16[256,512]{1,0:T(8,128)(2,1)}) %reduce-scatter.7.cloned.1.call-update) | async-done | bytes 262160 | tf_op jit(solution)/shard_map/reduce_scatter | solution.py:318
  816.7 42.5 %reduce-scatter.5.cloned.1.call-done = bf16[256,512]{1,0:T(8,128)(2,1)} async-done(((bf16[2048,512]{1,0:T(8,128)(2,1)}), bf16[256,512]{1,0:T(8,128)(2,1)}) %reduce-scatter.5.cloned.1.call-update) | async-done | bytes 262160 | tf_op jit(solution)/shard_map/reduce_scatter | solution.py:315
  (321 shorter events, 110.5 us)
Async XLA Ops:
  7.2 329.5 %copy-start = (bf16[2048,2,256]{2,1,0:T(2,128)(2,1)S(1)}, bf16[2048,2,256]{2,1,0:T(2,128)(2,1)}, u32[]{:S(2)}) copy-start(bf16[2048,2,256]{2,1,0:T(2,128)(2,1)} %param.26) | copy-start | bytes 6291460
  7.2 33.2 %all-gather.10.cloned.1.call-start = ((), (), s32[]{:S(2)}) async-start(), calls=%async_computation.8 | async-start | bytes 2359296 | tf_op jit(solution)/shard_map/all_gather | solution.py:119
  7.9 62.2 %all-gather.12.cloned.1.call-start = ((), (), s32[]{:S(2)}) async-start(), calls=%async_computation.9 | async-start | bytes 2359296 | tf_op jit(solution)/shard_map/all_gather | solution.py:120
  8.7 61.4 %copy-start.2 = (bf16[128,2048]{1,0:T(8,128)(2,1)S(1)}, bf16[128,2048]{1,0:T(8,128)(2,1)}, u32[]{:S(2)}) copy-start(bf16[128,2048]{1,0:T(8,128)(2,1)} %param.16) | copy-start | bytes 1572868
  8.7 61.4 %copy-start.32 = (f32[2048]{0:T(1024)S(1)}, f32[2048]{0:T(1024)}, u32[]{:S(2)}) copy-start(f32[2048]{0:T(1024)} %param.17) | copy-start | bytes 24580
  8.7 91.1 %all-gather.16.cloned.1.call-start = ((), (), s32[]{:S(2)}) async-start(), calls=%async_computation.11 | async-start | bytes 2359296 | tf_op jit(solution)/shard_map/all_gather | solution.py:121
  9.4 198.1 %all-gather.14.cloned.1.call-start = ((), (), s32[]{:S(2)}) async-start(), calls=%async_computation.10 | async-start | bytes 1179648 | tf_op jit(solution)/shard_map/all_gather | solution.py:141
  15.4 84.4 %copy-start.53 = (f32[128]{0:T(128)}, f32[128]{0:T(128)S(1)}, u32[]{:S(2)}) copy-start(f32[128]{0:T(128)S(1)} %get-tuple-element.122) | copy-start | bytes 1540
  42.8 45.6 %copy-start.14 = (f32[128,512]{1,0:T(8,128)}, f32[128,512]{1,0:T(8,128)S(1)}, u32[]{:S(2)}) copy-start(f32[128,512]{1,0:T(8,128)S(1)} %get-tuple-element.132) | copy-start | bytes 786436
  42.8 42.3 %copy-start.45 = (f32[512]{0:T(512)S(1)}, f32[512]{0:T(512)}, u32[]{:S(2)}) copy-start(f32[512]{0:T(512)} %param.22) | copy-start | bytes 6148
  42.8 44.1 %copy-start.43 = (f32[512]{0:T(512)S(1)}, f32[512]{0:T(512)}, u32[]{:S(2)}) copy-start(f32[512]{0:T(512)} %param.23) | copy-start | bytes 6148
  93.2 118.8 %all-gather.18.cloned.1.call-start = ((), (), s32[]{:S(2)}) async-start(), calls=%async_computation.12 | async-start | bytes 1179648 | tf_op jit(solution)/shard_map/all_gather | solution.py:142
  102.7 112.7 %all-gather.20.cloned.1.call-start = ((), (), s32[]{:S(2)}) async-start(), calls=%async_computation.13 | async-start | bytes 2359296 | tf_op jit(solution)/shard_map/all_gather | solution.py:122
  136.5 70.3 %copy-start.77 = (s32[4,1]{0,1:T(1,128)S(1)}, s32[4,1]{0,1:T(1,128)}, u32[]{:S(2)}) copy-start(s32[4,1]{0,1:T(1,128)} %copy-done.76) | copy-start | bytes 52
  136.5 70.4 %copy-start.71 = (s32[128]{0:T(128)S(1)}, s32[128]{0:T(128)}, u32[]{:S(2)}) copy-start(s32[128]{0:T(128)} %copy-done.70) | copy-start | bytes 1540
  136.5 70.9 %copy-start.26 = (bf16[128,4,64]{2,0,1:T(8,128)(2,1)S(1)}, bf16[128,4,64]{2,0,1:T(8,128)(2,1)}, u32[]{:S(2)}) copy-start(bf16[128,4,64]{2,0,1:T(8,128)(2,1)} %get-tuple-element.109) | copy-start | bytes 196612
  136.5 70.9 %copy-start.27 = (bf16[128,4,64]{2,0,1:T(8,128)(2,1)S(1)}, bf16[128,4,64]{2,0,1:T(8,128)(2,1)}, u32[]{:S(2)}) copy-start(bf16[128,4,64]{2,0,1:T(8,128)(2,1)} %get-tuple-element.110) | copy-start | bytes 196612
  136.6 134.6 %all-to-all-start.2 = ((bf16[16,72,2048]{2,1,0:T(8,128)(2,1)}), bf16[16,72,2048]{2,1,0:T(8,128)(2,1)}, u32[]{:S(2)}, u32[]{:S(2)}) async-start(bf16[16,72,2048]{2,1,0:T(8,128)(2,1)} %multiply_convert_fusion), calls=%async_computation.2 | async-start | bytes 9437184 | tf_op jit(solution)/shard_map/all_to_all | solution.py:176
  141.3 115.9 %all-reduce.14.cloned.1.call-start = ((), (), s32[]{:S(2)}) async-start(), calls=%async_computation.14 | async-start | bytes 1048576 | tf_op jit(solution)/shard_map/psum | solution.py:160
  215.4 43.2 %copy-start.28 = (bf16[128,4,128]{0,2,1:T(8,128)(2,1)}, bf16[128,4,128]{0,2,1:T(8,128)(2,1)S(1)}, u32[]{:S(2)}) copy-start(bf16[128,4,128]{0,2,1:T(8,128)(2,1)S(1)} %get-tuple-element.137) | copy-start | bytes 393220
  215.4 41.9 %copy-start.3 = (bf16[128,2048]{1,0:T(8,128)(2,1)S(1)}, bf16[128,2048]{1,0:T(8,128)(2,1)}, u32[]{:S(2)}) copy-start(bf16[128,2048]{1,0:T(8,128)(2,1)} %param.16) | copy-start | bytes 1572868
  215.4 43.6 %copy-start.34 = (f32[2048]{0:T(1024)S(1)}, f32[2048]{0:T(1024)}, u32[]{:S(2)}) copy-start(f32[2048]{0:T(1024)} %param.24) | copy-start | bytes 24580
  271.2 59.3 %all-to-all-start = ((bf16[16,72,2048]{2,1,0:T(8,128)(2,1)}), bf16[16,72,2048]{2,1,0:T(8,128)(2,1)}, u32[]{:S(2)}, u32[]{:S(2)}) async-start(bf16[16,72,2048]{2,1,0:T(8,128)(2,1)} %broadcast_multiply_fusion), calls=%async_computation | async-start | bytes 9437184 | tf_op jit(solution)/shard_map/all_to_all | solution.py:175
  353.8 59.8 %all-to-all-start.3 = ((bf16[2,576,2048]{2,0,1:T(2,128)(2,1)}), bf16[2,576,2048]{2,0,1:T(2,128)(2,1)}, u32[]{:S(2)}, u32[]{:S(2)}) async-start(bf16[2,576,2048]{2,0,1:T(2,128)(2,1)} %copy.183), calls=%async_computation.3 | async-start | bytes 9437184 | tf_op jit(solution)/shard_map/all_to_all | solution.py:197
  371.8 47.2 %copy-start.52 = (s32[1024,1]{0,1:T(1,128)S(1)}, s32[1024,1]{0,1:T(1,128)}, u32[]{:S(2)}) copy-start(s32[1024,1]{0,1:T(1,128)} %copy-done.51) | copy-start | bytes 12292
  371.8 47.2 %copy-start.38 = (s32[8,1,128]{2,1,0:T(1,128)S(1)}, s32[8,1,128]{2,1,0:T(1,128)}, u32[]{:S(2)}) copy-start(s32[8,1,128]{2,1,0:T(1,128)} %copy-done.37) | copy-start | bytes 12292
  371.8 47.2 %copy-start.40 = (s32[1024]{0:T(1024)S(1)}, s32[1024]{0:T(1024)}, u32[]{:S(2)}) copy-start(s32[1024]{0:T(1024)} %copy-done.39) | copy-start | bytes 12292
  371.8 47.3 %copy-start.61 = (s32[128]{0:T(128)S(1)}, s32[128]{0:T(128)}, u32[]{:S(2)}) copy-start(s32[128]{0:T(128)} %param.29) | copy-start | bytes 1540
  371.8 47.3 %copy-start.72 = (s32[128]{0:T(128)S(1)}, s32[128]{0:T(128)}, u32[]{:S(2)}) copy-start(s32[128]{0:T(128)} %copy-done.70) | copy-start | bytes 1540
  371.8 47.6 %copy-start.64 = (bf16[128,4]{0,1:T(4,128)(2,1)S(1)}, bf16[128,4]{0,1:T(4,128)(2,1)}, u32[]{:S(2)}) copy-start(bf16[128,4]{0,1:T(4,128)(2,1)} %get-tuple-element.113) | copy-start | bytes 3076
  413.6 98.2 %all-to-all-start.1 = ((bf16[2,576,2048]{2,0,1:T(2,128)(2,1)}), bf16[2,576,2048]{2,0,1:T(2,128)(2,1)}, u32[]{:S(2)}, u32[]{:S(2)}) async-start(bf16[2,576,2048]{2,0,1:T(2,128)(2,1)} %copy.176), calls=%async_computation.1 | async-start | bytes 9437184 | tf_op jit(solution)/shard_map/all_to_all | solution.py:194
  418.2 90.2 %all-gather.22.cloned.1.call-start = ((), (), s32[]{:S(2)}) async-start(), calls=%async_computation.16 | async-start | bytes 1179648 | tf_op jit(solution)/shard_map/all_gather | solution.py:244
  419.0 126.2 %all-reduce.16.cloned.1.call-start = ((), (), s32[]{:S(2)}) async-start(), calls=%async_computation.15 | async-start | bytes 1048576 | tf_op jit(solution)/shard_map/psum | solution.py:211
  508.3 82.3 %all-gather.24.cloned.1.call-start = ((), (), s32[]{:S(2)}) async-start(), calls=%async_computation.17 | async-start | bytes 1179648 | tf_op jit(solution)/shard_map/all_gather | solution.py:247
  511.7 33.5 %copy-start.57 = (f32[128]{0:T(128)S(1)}, f32[128]{0:T(128)}, u32[]{:S(2)}) copy-start(f32[128]{0:T(128)} %copy-done.56) | copy-start | bytes 1540
  511.7 35.5 %copy-start.8 = (bf16[128,2048]{1,0:T(8,128)(2,1)S(1)}, bf16[128,2048]{1,0:T(8,128)(2,1)}, u32[]{:S(2)}) copy-start(bf16[128,2048]{1,0:T(8,128)(2,1)} %param.31) | copy-start | bytes 1572868
  511.7 35.5 %copy-start.67 = (f32[128]{0:T(128)S(1)}, f32[128]{0:T(128)}, u32[]{:S(2)}) copy-start(f32[128]{0:T(128)} %get-tuple-element.129) | copy-start | bytes 1540
  550.4 132.2 %all-reduce.18.cloned.1.call-start = ((), (), s32[]{:S(2)}) async-start(), calls=%async_computation.22 | async-start | bytes 2097152 | tf_op jit(solution)/shard_map/psum | solution.py:210
  633.2 92.9 %reduce-scatter.11.cloned.1.call-start = ((), (), s32[]{:S(2)}) async-start(), calls=%async_computation.21 | async-start | bytes 2359296 | tf_op jit(solution)/shard_map/reduce_scatter | solution.py:324
  636.5 134.1 %reduce-scatter.9.cloned.1.call-start = ((), (), s32[]{:S(2)}) async-start(), calls=%async_computation.20 | async-start | bytes 2359296 | tf_op jit(solution)/shard_map/reduce_scatter | solution.py:321
  639.4 175.5 %reduce-scatter.7.cloned.1.call-start = ((), (), s32[]{:S(2)}) async-start(), calls=%async_computation.19 | async-start | bytes 2359296 | tf_op jit(solution)/shard_map/reduce_scatter | solution.py:318
  641.7 217.5 %reduce-scatter.5.cloned.1.call-start = ((), (), s32[]{:S(2)}) async-start(), calls=%async_computation.18 | async-start | bytes 2359296 | tf_op jit(solution)/shard_map/reduce_scatter | solution.py:315
  672.8 38.0 %copy-start.55 = (f32[128]{0:T(128)S(1)}, f32[128]{0:T(128)}, u32[]{:S(2)}) copy-start(f32[128]{0:T(128)} %copy-done.53) | copy-start | bytes 1540
  672.8 38.0 %copy-start.59 = (f32[128]{0:T(128)S(1)}, f32[128]{0:T(128)}, u32[]{:S(2)}) copy-start(f32[128]{0:T(128)} %copy-done.56) | copy-start | bytes 1540
  672.8 38.0 %copy-start.69 = (f32[128]{0:T(128)S(1)}, f32[128]{0:T(128)}, u32[]{:S(2)}) copy-start(f32[128]{0:T(128)} %get-tuple-element.129) | copy-start | bytes 1540
  672.9 38.0 %copy-start.74 = (f32[128]{0:T(128)S(1)}, f32[128]{0:T(128)}, u32[]{:S(2)}) copy-start(f32[128]{0:T(128)} %copy-done.73) | copy-start | bytes 1540
  672.9 38.0 %copy-start.75 = (f32[128]{0:T(128)S(1)}, f32[128]{0:T(128)}, u32[]{:S(2)}) copy-start(f32[128]{0:T(128)} %get-tuple-element.121) | copy-start | bytes 1540
  710.8 150.1 %copy-start.1 = (bf16[2048,2,256]{2,1,0:T(2,128)(2,1)S(1)}, bf16[2048,2,256]{2,1,0:T(2,128)(2,1)}, u32[]{:S(2)}) copy-start(bf16[2048,2,256]{2,1,0:T(2,128)(2,1)} %param.26) | copy-start | bytes 6291460
  (57 other events, 362.6 us)
Sparse Core Ops, SparseCore 0:
  9.9 30.4 all-gather.9
  42.3 27.7 all-gather.11
  72.0 27.7 all-gather.15
  102.2 23.3 all-gather.13
  127.9 26.3 all-gather.17
  156.0 52.6 all-gather.19
  218.9 38.3 all-reduce.13
  420.9 35.1 all-gather.21
  508.5 36.7 all-reduce.15
  550.5 23.2 all-gather.23
  633.3 49.2 all-reduce.17
  685.8 40.3 reduce-scatter.10
  729.4 41.1 reduce-scatter.8
  773.7 41.1 reduce-scatter.6
  818.0 41.1 reduce-scatter.4
where the time goes:
time: 877 us; the launch traced here: 868 us
  waiting for transfers between devices  360 us (41%)
  blocking collectives  190 us (22%)
  local copies, waits for them, and re-layouts  129 us (15%)
  other arithmetic  83.5 us (10%)
  matrix products  69.1 us (8%)
  starting transfers between devices  20.1 us (2%)
  between operations  16.2 us (2%)
    all_gather x1, blocking collectives, shards(): anchor_piece = lax.all_gather(anchor, 'dp', axis=0, tiled=True)  65.4 us
    all_gather x1, blocking collectives, shards(): lax.all_gather(log_total.T.astype(jnp.bfloat16), 'dp', axis=0, tiled=True)  60.7 us
    all_to_all x1, waiting for transfers between devices, shards(): lax.all_to_all(buffer_rows, 'dp', split_axis=0, concat_axis=1, tiled=True)  49.4 us
    reduce_scatter x1, waiting for transfers between devices, shards(): lax.psum_scatter(grad_value_w.astype(jnp.bfloat16), 'dp', scatter_dimensi...  42.6 us
    reduce_scatter x1, waiting for transfers between devices, shards(): lax.psum_scatter(grad_key_w.astype(jnp.bfloat16), 'dp', scatter_dimension...  42.5 us
    reduce_scatter x1, waiting for transfers between devices, shards(): lax.psum_scatter(grad_query_w.astype(jnp.bfloat16), 'dp', scatter_dimensi...  42.5 us
    all_to_all x1, waiting for transfers between devices, shards(): lax.all_to_all(grad_buffer.astype(jnp.bfloat16), 'dp', split_axis=1, conc...  41.7 us
    psum x1, waiting for transfers between devices, shards(): lax.psum(contract_last(attended_low, output_full).astype(jnp.bfloat16), '...  38.4 us
  transfers between devices with their start and end apart: 19, of which 12 were waited for; matrix products, arithmetic and copies ran while one was open for 26% of the time, Pallas kernels for 0%

commit v1 on v0

--- a/solution.py
+++ b/solution.py
@@ -208,7 +208,9 @@
     grad_moe_part = jnp.sum(grad_table[dest_rows].reshape(tok_rows, TOPK, width), axis=1)
     moe_sum, grad_moe_in = (
         lax.psum(combined.astype(jnp.bfloat16), "tensor").astype(jnp.float32),
-        lax.psum(grad_moe_part.astype(jnp.bfloat16), "tensor").astype(jnp.float32),
+        jnp.sum(lax.all_gather(grad_moe_part.astype(jnp.bfloat16), "tensor"), axis=0).astype(
+            jnp.float32
+        ),
     )
     output = (residual + moe_sum).astype(bf16)
     query_full, key_full, value_full, output_full = (

time: 877 us -> 828 us (0.944)
  blocking collectives: 190 us -> 157 us
  waiting for transfers between devices: 360 us -> 344 us
    all_gather x1, blocking collectives: 60.7 us -> 28.7 us  [shards(): lax.all_gather(log_total.T.astype(jnp.bfloat16), 'dp', axis=0, tiled=True)]
    psum x1 -> x0, waiting for transfers between devices: 26.7 us -> none  [shards(): lax.psum(grad_moe_part.astype(jnp.bfloat16), 'tensor').astype(jnp.float32)]
    unnamed x177 -> x179, local copies, waits for them, and re-layouts: 28.1 us -> 28.1 us
  transfers between devices with their start and end apart: 19 -> 19, of which waited for: 12 -> 12; matrix products, arithmetic and copies ran while one was open for 26% -> 27% of each run, Pallas kernels for 0% -> 0%
where the time goes in v1:
time: 828 us; the launch traced here: 819 us
  waiting for transfers between devices  344 us (42%)
  blocking collectives  157 us (19%)
  local copies, waits for them, and re-layouts  129 us (16%)
  other arithmetic  84.5 us (10%)
  matrix products  68.9 us (8%)
  starting transfers between devices  20.4 us (2%)
  between operations  16.2 us (2%)
    all_gather x1, blocking collectives, shards(): anchor_piece = lax.all_gather(anchor, 'dp', axis=0, tiled=True)  65.4 us
    all_to_all x1, waiting for transfers between devices, shards(): lax.all_to_all(buffer_rows, 'dp', split_axis=0, concat_axis=1, tiled=True)  49.5 us
    all_to_all x1, waiting for transfers between devices, shards(): lax.all_to_all(grad_buffer.astype(jnp.bfloat16), 'dp', split_axis=1, conc...  45.2 us
    reduce_scatter x1, waiting for transfers between devices, shards(): lax.psum_scatter(grad_value_w.astype(jnp.bfloat16), 'dp', scatter_dimensi...  42.6 us
    reduce_scatter x1, waiting for transfers between devices, shards(): lax.psum_scatter(grad_key_w.astype(jnp.bfloat16), 'dp', scatter_dimension...  42.5 us
    reduce_scatter x1, waiting for transfers between devices, shards(): lax.psum_scatter(grad_query_w.astype(jnp.bfloat16), 'dp', scatter_dimensi...  42.5 us
    psum x1, waiting for transfers between devices, shards(): lax.psum(contract_last(attended_low, output_full).astype(jnp.bfloat16), '...  38.4 us
    all_gather x1, blocking collectives, shards(): lax.all_gather(log_total.T.astype(jnp.bfloat16), 'dp', axis=0, tiled=True)  28.7 us
  transfers between devices with their start and end apart: 19, of which 12 were waited for; matrix products, arithmetic and copies ran while one was open for 27% of the time, Pallas kernels for 0%

profile of v1, /device:TPU:0, one launch (start us, length us, event | category | flops | bytes accessed | tf_op | source)
XLA Modules:
  0.0 819.3 jit_solution(13346800134732422109)
XLA Ops:
  15.4 25.0 %all-gather.12.cloned.1.call-done = bf16[2048,512]{1,0:T(8,128)(2,1)} async-done(((bf16[256,512]{1,0:T(8,128)(2,1)}), bf16[2048,512]{1,0:T(8,128)(2,1)}) %all-gather.12.cloned.1.call-update) | async-done | bytes 2097168 | tf_op jit(solution)/shard_map/all_gather | solution.py:119
  42.8 27.3 %all-gather.14.cloned.1.call-done = bf16[2048,512]{1,0:T(8,128)(2,1)} async-done(((bf16[256,512]{1,0:T(8,128)(2,1)}), bf16[2048,512]{1,0:T(8,128)(2,1)}) %all-gather.14.cloned.1.call-update) | async-done | bytes 2097168 | tf_op jit(solution)/shard_map/all_gather | solution.py:120
  72.3 11.7 %all-reduce.7 = (f32[128]{0:T(128)S(1)}, f32[128]{0:T(128)S(1)}) all-reduce(f32[128]{0:T(128)S(1)} %get-tuple-element.131, f32[128]{0:T(128)S(1)} %get-tuple-element.133), channel_id=1, replica_groups=mesh['dp'=8,'tensor'=4] {'tensor'}, use_global_device_ids=true, to_apply=%region_5.6 | all-reduce | flops 256 | bytes 2048 | tf_op jit(solution)/shard_map/psum | solution.py:127
  93.3 6.5 all-gather.18.cloned.1.call-done
  103.5 4.5 reduce-window.19
  109.0 4.3 scatter_custom_fusion
  113.3 4.3 scatter_custom_fusion.1
  117.7 4.3 scatter_custom_fusion.2
  123.3 6.8 gather_fusion.2
  130.1 6.5 multiply_convert_fusion
  136.6 4.8 all-to-all-start.2
  141.4 65.4 %all-gather.1 = s32[8,1,128]{2,1,0:T(1,128)S(1)} all-gather(s32[1,1,128]{2,1,0:T(1,128)S(1)} %bitcast.189), channel_id=1, replica_groups=mesh['dp'=8,'tensor'=4] {'dp'}, dimensions={0}, use_global_device_ids=true | all-gather | bytes 4608 | tf_op jit(solution)/shard_map/all_gather | solution.py:143
  218.9 38.4 %all-reduce.13.cloned.1.call-done = bf16[128,2048]{1,0:T(8,128)(2,1)} async-done(((bf16[128,2048]{1,0:T(8,128)(2,1)}), bf16[128,2048]{1,0:T(8,128)(2,1)}) %all-reduce.13.cloned.1.call-update) | async-done | bytes 524304 | tf_op jit(solution)/shard_map/psum | solution.py:160
  260.3 5.9 gather_fusion
  266.3 4.9 broadcast_multiply_fusion
  271.2 4.6 all-to-all-start
  275.8 5.3 copy.180
  281.0 49.5 %all-to-all-done = bf16[16,72,2048]{2,1,0:T(8,128)(2,1)} async-done(((bf16[16,72,2048]{2,1,0:T(8,128)(2,1)}), bf16[16,72,2048]{2,1,0:T(8,128)(2,1)}, u32[]{:S(2)}, u32[]{:S(2)}) %all-to-all-start) | async-done | bytes 4718624 | tf_op jit(solution)/shard_map/all_to_all | solution.py:175
  340.2 4.3 bitcast_convert_fusion
  344.5 9.4 %copy.183 = bf16[2,576,2048]{2,0,1:T(2,128)(2,1)} copy(bf16[2,576,2048]{2,1,0:T(8,128)(2,1)} %bitcast_convert_fusion) | data formatting | bytes 9437184 | tf_op jit(solution)/shard_map/convert_element_type | solution.py:198
  353.8 4.8 all-to-all-start.3
  359.4 3.6 convolution_convert_fusion
  363.0 9.3 %copy.176 = bf16[2,576,2048]{2,0,1:T(2,128)(2,1)} copy(bf16[2,576,2048]{2,1,0:T(8,128)(2,1)} %convolution_convert_fusion) | data formatting | bytes 9437184 | tf_op jit(solution)/shard_map/convert_element_type | solution.py:195
  372.3 45.2 %all-to-all-done.3 = bf16[2,576,2048]{2,0,1:T(2,128)(2,1)} async-done(((bf16[2,576,2048]{2,0,1:T(2,128)(2,1)}), bf16[2,576,2048]{2,0,1:T(2,128)(2,1)}, u32[]{:S(2)}, u32[]{:S(2)}) %all-to-all-start.3) | async-done | bytes 4718624 | tf_op jit(solution)/shard_map/all_to_all | solution.py:197
  417.5 4.6 all-to-all-start.1
  422.4 4.5 copy.184
  426.9 5.0 pad_convert_fusion
  431.8 12.6 %gather_fusion.3 = f32[1024,2048]{1,0:T(8,128)} fusion(f32[1153,2048]{1,0:T(8,128)} %pad_convert_fusion, s32[1024]{0:T(1024)S(1)} %broadcast_clamp_fusion), kind=kCustom, calls=%fused_computation.3 | custom fusion | bytes 16781312 | tf_op jit(solution)/shard_map/gather | solution.py:208
  444.4 6.2 bitcast_reduce_fusion
  451.1 28.7 %all_gather.54 = bf16[1024,4]{0,1:T(4,128)(2,1)S(1)} all-gather(bf16[128,4]{0,1:T(4,128)(2,1)S(1)} %copy-done.65), channel_id=1, replica_groups=mesh['dp'=8,'tensor'=4] {'dp'}, dimensions={0}, use_global_device_ids=true | all-gather | bytes 9216 | tf_op jit(solution)/shard_map/all_gather | solution.py:252
  483.2 6.7 copy.177
  489.9 6.8 all-gather.28.cloned.1.call-done
  503.0 7.3 pad_convert_fusion.1
  510.3 12.6 %gather_fusion.1 = f32[1024,2048]{1,0:T(8,128)} fusion(f32[1153,2048]{1,0:T(8,128)} %pad_convert_fusion.1, s32[1024]{0:T(1024)S(1)} %broadcast_clamp_fusion), kind=kCustom, calls=%fused_computation.1 | custom fusion | bytes 16781312 | tf_op jit(solution)/shard_map/gather | solution.py:205
  522.8 7.5 fusion
  530.4 8.9 %all_gather.56 = bf16[1024,4]{0,1:T(4,128)(2,1)S(1)} all-gather(bf16[128,4]{0,1:T(4,128)(2,1)S(1)} %convert_element_type.269), channel_id=1, replica_groups=mesh['dp'=8,'tensor'=4] {'dp'}, dimensions={0}, use_global_device_ids=true | all-gather | bytes 9216 | tf_op jit(solution)/shard_map/all_gather | solution.py:255
  539.3 3.6 fusion.22
  557.5 18.1 %all-reduce.6 = (f32[128]{0:T(128)}, f32[128]{0:T(128)S(1)}, bf16[2048]{0:T(1024)(128)(2,1)}, bf16[2048]{0:T(1024)(128)(2,1)}) all-reduce(f32[128]{0:T(128)S(1)} %get-tuple-element.79, f32[128]{0:T(128)} %get-tuple-element.77, f32[2048]{0:T(1024)S(1)} %dynamic_update_slice.6, ...), channel_id=1, replica_groups=mesh['dp'=8,'tensor'=4] {'tensor'}, use_global_device_ids=true, to_apply=%region_26.27 | all-reduce | flops 4352 | bytes 26624 | tf_op jit(solution)/shard_map/psum | solution.py:289
  596.6 8.2 convolution_bitcast_fusion
  604.8 13.3 %copy.195 = f32[2048,2,2,256]{3,2,1,0:T(2,128)} copy(f32[2048,2,2,256]{0,3,2,1:T(8,128)} %convolution_bitcast_fusion) | data formatting | bytes 16777216
  618.0 6.2 convolution_bitcast_fusion.1
  624.3 7.2 copy.196
  635.4 24.2 %all-reduce.8 = (bf16[2048]{0:T(1024)(128)(2,1)S(1)}, bf16[2048]{0:T(1024)(128)(2,1)S(1)}, bf16[2048]{0:T(1024)(128)(2,1)S(1)}, bf16[2048]{0:T(1024)(128)(2,1)S(1)}) all-reduce(bf16[2048]{0:T(1024)(128)(2,1)S(1)} %get-tuple-element.74, bf16[2048]{0:T(1024)(128)(2,1)S(1)} %copy-done.66, ...), channel_id=7, replica_groups=mesh['dp'=8,'tensor'=4] {'dp'}, use_global_device_ids=true, to_apply=%region_36.37.clone | all-reduce | flops 8192 | bytes 32768
  662.3 3.7 fusion.24
  665.9 11.6 %reduce-scatter.11.cloned.1.call-done = bf16[256,512]{1,0:T(8,128)(2,1)} async-done(((bf16[2048,512]{1,0:T(8,128)(2,1)}), bf16[256,512]{1,0:T(8,128)(2,1)}) %reduce-scatter.11.cloned.1.call-update) | async-done | bytes 262160 | tf_op jit(solution)/shard_map/reduce_scatter | solution.py:326
  679.4 42.6 %reduce-scatter.9.cloned.1.call-done = bf16[256,512]{1,0:T(8,128)(2,1)} async-done(((bf16[2048,512]{1,0:T(8,128)(2,1)}), bf16[256,512]{1,0:T(8,128)(2,1)}) %reduce-scatter.9.cloned.1.call-update) | async-done | bytes 262160 | tf_op jit(solution)/shard_map/reduce_scatter | solution.py:323
  723.8 42.5 %reduce-scatter.7.cloned.1.call-done = bf16[256,512]{1,0:T(8,128)(2,1)} async-done(((bf16[2048,512]{1,0:T(8,128)(2,1)}), bf16[256,512]{1,0:T(8,128)(2,1)}) %reduce-scatter.7.cloned.1.call-update) | async-done | bytes 262160 | tf_op jit(solution)/shard_map/reduce_scatter | solution.py:320
  768.1 42.5 %reduce-scatter.5.cloned.1.call-done = bf16[256,512]{1,0:T(8,128)(2,1)} async-done(((bf16[2048,512]{1,0:T(8,128)(2,1)}), bf16[256,512]{1,0:T(8,128)(2,1)}) %reduce-scatter.5.cloned.1.call-update) | async-done | bytes 262160 | tf_op jit(solution)/shard_map/reduce_scatter | solution.py:317
  (324 shorter events, 111.7 us)
Async XLA Ops:
  7.2 329.5 %copy-start = (bf16[2048,2,256]{2,1,0:T(2,128)(2,1)S(1)}, bf16[2048,2,256]{2,1,0:T(2,128)(2,1)}, u32[]{:S(2)}) copy-start(bf16[2048,2,256]{2,1,0:T(2,128)(2,1)} %param.26) | copy-start | bytes 6291460
  7.2 33.2 %all-gather.12.cloned.1.call-start = ((), (), s32[]{:S(2)}) async-start(), calls=%async_computation.8 | async-start | bytes 2359296 | tf_op jit(solution)/shard_map/all_gather | solution.py:119
  7.9 62.2 %all-gather.14.cloned.1.call-start = ((), (), s32[]{:S(2)}) async-start(), calls=%async_computation.9 | async-start | bytes 2359296 | tf_op jit(solution)/shard_map/all_gather | solution.py:120
  8.7 61.4 %copy-start.2 = (bf16[128,2048]{1,0:T(8,128)(2,1)S(1)}, bf16[128,2048]{1,0:T(8,128)(2,1)}, u32[]{:S(2)}) copy-start(bf16[128,2048]{1,0:T(8,128)(2,1)} %param.16) | copy-start | bytes 1572868
  8.7 61.4 %copy-start.33 = (f32[2048]{0:T(1024)S(1)}, f32[2048]{0:T(1024)}, u32[]{:S(2)}) copy-start(f32[2048]{0:T(1024)} %param.17) | copy-start | bytes 24580
  8.7 91.1 %all-gather.18.cloned.1.call-start = ((), (), s32[]{:S(2)}) async-start(), calls=%async_computation.11 | async-start | bytes 2359296 | tf_op jit(solution)/shard_map/all_gather | solution.py:121
  9.4 198.1 %all-gather.16.cloned.1.call-start = ((), (), s32[]{:S(2)}) async-start(), calls=%async_computation.10 | async-start | bytes 1179648 | tf_op jit(solution)/shard_map/all_gather | solution.py:141
  15.4 84.4 %copy-start.54 = (f32[128]{0:T(128)}, f32[128]{0:T(128)S(1)}, u32[]{:S(2)}) copy-start(f32[128]{0:T(128)S(1)} %get-tuple-element.122) | copy-start | bytes 1540
  42.8 45.6 %copy-start.15 = (f32[128,512]{1,0:T(8,128)}, f32[128,512]{1,0:T(8,128)S(1)}, u32[]{:S(2)}) copy-start(f32[128,512]{1,0:T(8,128)S(1)} %get-tuple-element.132) | copy-start | bytes 786436
  42.8 42.3 %copy-start.46 = (f32[512]{0:T(512)S(1)}, f32[512]{0:T(512)}, u32[]{:S(2)}) copy-start(f32[512]{0:T(512)} %param.22) | copy-start | bytes 6148
  42.8 44.2 %copy-start.44 = (f32[512]{0:T(512)S(1)}, f32[512]{0:T(512)}, u32[]{:S(2)}) copy-start(f32[512]{0:T(512)} %param.23) | copy-start | bytes 6148
  72.3 19.4 %copy-start.17 = (f32[128,512]{1,0:T(8,128)}, f32[128,512]{1,0:T(8,128)S(1)}, u32[]{:S(2)}) copy-start(f32[128,512]{1,0:T(8,128)S(1)} %get-tuple-element.134) | copy-start | bytes 786436
  93.3 15.5 %copy-start.64 = (f32[128,8]{0,1:T(8,128)S(1)}, f32[128,8]{0,1:T(8,128)}, u32[]{:S(2)}) copy-start(f32[128,8]{0,1:T(8,128)} %param.28) | copy-start | bytes 12292
  93.3 118.7 %all-gather.20.cloned.1.call-start = ((), (), s32[]{:S(2)}) async-start(), calls=%async_computation.12 | async-start | bytes 1179648 | tf_op jit(solution)/shard_map/all_gather | solution.py:142
  102.7 112.7 %all-gather.22.cloned.1.call-start = ((), (), s32[]{:S(2)}) async-start(), calls=%async_computation.13 | async-start | bytes 2359296 | tf_op jit(solution)/shard_map/all_gather | solution.py:122
  136.5 70.3 %copy-start.78 = (s32[4,1]{0,1:T(1,128)S(1)}, s32[4,1]{0,1:T(1,128)}, u32[]{:S(2)}) copy-start(s32[4,1]{0,1:T(1,128)} %copy-done.77) | copy-start | bytes 52
  136.5 70.4 %copy-start.72 = (s32[128]{0:T(128)S(1)}, s32[128]{0:T(128)}, u32[]{:S(2)}) copy-start(s32[128]{0:T(128)} %copy-done.71) | copy-start | bytes 1540
  136.5 70.9 %copy-start.27 = (bf16[128,4,64]{2,0,1:T(8,128)(2,1)S(1)}, bf16[128,4,64]{2,0,1:T(8,128)(2,1)}, u32[]{:S(2)}) copy-start(bf16[128,4,64]{2,0,1:T(8,128)(2,1)} %get-tuple-element.109) | copy-start | bytes 196612
  136.6 70.9 %copy-start.28 = (bf16[128,4,64]{2,0,1:T(8,128)(2,1)S(1)}, bf16[128,4,64]{2,0,1:T(8,128)(2,1)}, u32[]{:S(2)}) copy-start(bf16[128,4,64]{2,0,1:T(8,128)(2,1)} %get-tuple-element.110) | copy-start | bytes 196612
  136.6 134.6 %all-to-all-start.2 = ((bf16[16,72,2048]{2,1,0:T(8,128)(2,1)}), bf16[16,72,2048]{2,1,0:T(8,128)(2,1)}, u32[]{:S(2)}, u32[]{:S(2)}) async-start(bf16[16,72,2048]{2,1,0:T(8,128)(2,1)} %multiply_convert_fusion), calls=%async_computation.2 | async-start | bytes 9437184 | tf_op jit(solution)/shard_map/all_to_all | solution.py:176
  141.3 115.9 %all-reduce.13.cloned.1.call-start = ((), (), s32[]{:S(2)}) async-start(), calls=%async_computation.14 | async-start | bytes 1048576 | tf_op jit(solution)/shard_map/psum | solution.py:160
  215.4 43.2 %copy-start.29 = (bf16[128,4,128]{0,2,1:T(8,128)(2,1)}, bf16[128,4,128]{0,2,1:T(8,128)(2,1)S(1)}, u32[]{:S(2)}) copy-start(bf16[128,4,128]{0,2,1:T(8,128)(2,1)S(1)} %get-tuple-element.137) | copy-start | bytes 393220
  215.4 41.9 %copy-start.3 = (bf16[128,2048]{1,0:T(8,128)(2,1)S(1)}, bf16[128,2048]{1,0:T(8,128)(2,1)}, u32[]{:S(2)}) copy-start(bf16[128,2048]{1,0:T(8,128)(2,1)} %param.16) | copy-start | bytes 1572868
  215.4 43.6 %copy-start.35 = (f32[2048]{0:T(1024)S(1)}, f32[2048]{0:T(1024)}, u32[]{:S(2)}) copy-start(f32[2048]{0:T(1024)} %param.24) | copy-start | bytes 24580
  271.2 59.3 %all-to-all-start = ((bf16[16,72,2048]{2,1,0:T(8,128)(2,1)}), bf16[16,72,2048]{2,1,0:T(8,128)(2,1)}, u32[]{:S(2)}, u32[]{:S(2)}) async-start(bf16[16,72,2048]{2,1,0:T(8,128)(2,1)} %broadcast_multiply_fusion), calls=%async_computation | async-start | bytes 9437184 | tf_op jit(solution)/shard_map/all_to_all | solution.py:175
  339.2 20.2 %copy-start.13 = (bf16[2,576,256]{2,1,0:T(8,128)(2,1)}, bf16[2,576,256]{2,1,0:T(8,128)(2,1)S(1)}, u32[]{:S(2)}) copy-start(bf16[2,576,256]{2,1,0:T(8,128)(2,1)S(1)} %get-tuple-element.94) | copy-start | bytes 1769476
  353.8 63.7 %all-to-all-start.3 = ((bf16[2,576,2048]{2,0,1:T(2,128)(2,1)}), bf16[2,576,2048]{2,0,1:T(2,128)(2,1)}, u32[]{:S(2)}, u32[]{:S(2)}) async-start(bf16[2,576,2048]{2,0,1:T(2,128)(2,1)} %copy.183), calls=%async_computation.3 | async-start | bytes 9437184 | tf_op jit(solution)/shard_map/all_to_all | solution.py:197
  358.6 121.3 %all-gather.24.cloned.1.call-start = ((), (), s32[]{:S(2)}) async-start(), calls=%async_computation.15 | async-start | bytes 1179648 | tf_op jit(solution)/shard_map/all_gather | solution.py:246
  417.5 65.6 %all-to-all-start.1 = ((bf16[2,576,2048]{2,0,1:T(2,128)(2,1)}), bf16[2,576,2048]{2,0,1:T(2,128)(2,1)}, u32[]{:S(2)}, u32[]{:S(2)}) async-start(bf16[2,576,2048]{2,0,1:T(2,128)(2,1)} %copy.176), calls=%async_computation.1 | async-start | bytes 9437184 | tf_op jit(solution)/shard_map/all_to_all | solution.py:194
  422.2 74.5 %all-gather.28.cloned.1.call-start = ((), (), s32[]{:S(2)}) async-start(), calls=%async_computation.21 | async-start | bytes 2621440 | tf_op jit(solution)/shard_map/all_gather | solution.py:211
  444.4 35.5 %copy-start.43 = (f32[4,128]{1,0:T(4,128)S(1)}, f32[4,128]{1,0:T(4,128)}, u32[]{:S(2)}) copy-start(f32[4,128]{1,0:T(4,128)} %copy-done.42) | copy-start | bytes 6148
  444.4 35.4 %copy-start.49 = (f32[4,128]{1,0:T(4,128)S(1)}, f32[4,128]{1,0:T(4,128)}, u32[]{:S(2)}) copy-start(f32[4,128]{1,0:T(4,128)} %copy-done.48) | copy-start | bytes 6148
  444.4 35.5 %copy-start.26 = (bf16[128,4,128]{2,0,1:T(8,128)(2,1)S(1)}, bf16[128,4,128]{2,0,1:T(8,128)(2,1)}, u32[]{:S(2)}) copy-start(bf16[128,4,128]{2,0,1:T(8,128)(2,1)} %pad_maximum_fusion.4) | copy-start | bytes 393220
  450.7 92.3 %all-gather.26.cloned.1.call-start = ((), (), s32[]{:S(2)}) async-start(), calls=%async_computation.16 | async-start | bytes 1179648 | tf_op jit(solution)/shard_map/all_gather | solution.py:249
  502.8 131.3 %all-reduce.15.cloned.1.call-start = ((), (), s32[]{:S(2)}) async-start(), calls=%async_computation.22 | async-start | bytes 2097152 | tf_op jit(solution)/shard_map/psum | solution.py:210
  522.8 16.4 %copy-start.6 = (f32[4,128,1024]{2,1,0:T(8,128)S(1)}, f32[4,128,1024]{2,1,0:T(8,128)}, u32[]{:S(2)}) copy-start(f32[4,128,1024]{2,1,0:T(8,128)} %copy-done.5) | copy-start | bytes 6291460
  548.1 29.9 %copy-start.7 = (f32[4,1024,128]{2,1,0:T(8,128)S(1)}, f32[4,1024,128]{2,1,0:T(8,128)}, u32[]{:S(2)}) copy-start(f32[4,1024,128]{2,1,0:T(8,128)} %exponential_select_fusion) | copy-start | bytes 6291460
  584.6 93.0 %reduce-scatter.11.cloned.1.call-start = ((), (), s32[]{:S(2)}) async-start(), calls=%async_computation.20 | async-start | bytes 2359296 | tf_op jit(solution)/shard_map/reduce_scatter | solution.py:326
  587.9 134.1 %reduce-scatter.9.cloned.1.call-start = ((), (), s32[]{:S(2)}) async-start(), calls=%async_computation.19 | async-start | bytes 2359296 | tf_op jit(solution)/shard_map/reduce_scatter | solution.py:323
  590.8 175.5 %reduce-scatter.7.cloned.1.call-start = ((), (), s32[]{:S(2)}) async-start(), calls=%async_computation.18 | async-start | bytes 2359296 | tf_op jit(solution)/shard_map/reduce_scatter | solution.py:320
  593.1 217.5 %reduce-scatter.5.cloned.1.call-start = ((), (), s32[]{:S(2)}) async-start(), calls=%async_computation.17 | async-start | bytes 2359296 | tf_op jit(solution)/shard_map/reduce_scatter | solution.py:317
  604.8 13.3 %copy-start.14 = (bf16[2,576,256]{2,1,0:T(8,128)(2,1)S(1)}, bf16[2,576,256]{2,1,0:T(8,128)(2,1)}, u32[]{:S(2)}) copy-start(bf16[2,576,256]{2,1,0:T(8,128)(2,1)} %copy-done.13) | copy-start | bytes 1769476
  624.2 38.0 %copy-start.56 = (f32[128]{0:T(128)S(1)}, f32[128]{0:T(128)}, u32[]{:S(2)}) copy-start(f32[128]{0:T(128)} %copy-done.54) | copy-start | bytes 1540
  624.2 38.0 %copy-start.60 = (f32[128]{0:T(128)S(1)}, f32[128]{0:T(128)}, u32[]{:S(2)}) copy-start(f32[128]{0:T(128)} %copy-done.57) | copy-start | bytes 1540
  624.2 38.0 %copy-start.70 = (f32[128]{0:T(128)S(1)}, f32[128]{0:T(128)}, u32[]{:S(2)}) copy-start(f32[128]{0:T(128)} %get-tuple-element.129) | copy-start | bytes 1540
  624.3 38.0 %copy-start.75 = (f32[128]{0:T(128)S(1)}, f32[128]{0:T(128)}, u32[]{:S(2)}) copy-start(f32[128]{0:T(128)} %copy-done.74) | copy-start | bytes 1540
  624.3 38.0 %copy-start.76 = (f32[128]{0:T(128)S(1)}, f32[128]{0:T(128)}, u32[]{:S(2)}) copy-start(f32[128]{0:T(128)} %get-tuple-element.121) | copy-start | bytes 1540
  662.3 150.1 %copy-start.1 = (bf16[2048,2,256]{2,1,0:T(2,128)(2,1)S(1)}, bf16[2048,2,256]{2,1,0:T(2,128)(2,1)}, u32[]{:S(2)}) copy-start(bf16[2048,2,256]{2,1,0:T(2,128)(2,1)} %param.26) | copy-start | bytes 6291460
  (58 other events, 259.7 us)
Sparse Core Ops, SparseCore 0:
  9.9 30.4 all-gather.11
  42.3 27.7 all-gather.13
  72.0 27.7 all-gather.17
  102.2 23.3 all-gather.15
  127.9 26.3 all-gather.19
  156.0 52.6 all-gather.21
  218.9 38.3 all-reduce.12
  361.3 35.1 all-gather.23
  450.8 45.8 all-gather.27
  502.9 22.2 all-gather.25
  584.7 49.2 all-reduce.14
  637.2 40.3 reduce-scatter.10
  680.8 41.1 reduce-scatter.8
  725.1 41.1 reduce-scatter.6
  769.4 41.1 reduce-scatter.4
